TPU v7x, 32 devices: a whole 2x2x4 slice. The times are simulated.
32 devices in a mesh: fsdp: 8 (over z, y), dp: 4 (over x, core).
Axes of the slice: x: 2, y: 2, z: 4, core: 2. Of those that a mesh axis runs over, the one named last changes fastest.
Arguments:
- tokens: bfloat16 [32, 128, 3584], P(('fsdp', 'dp')), may hold values from -6 to 6
- lengths: int32 [32], P(('fsdp', 'dp')), may hold values from 32 to 128
- partner: int32 [32], replicated, may hold values from 0 to 31, as said below
- pair_weight: float32 [32], P(('fsdp', 'dp')), may hold values from 0.25 to 27
- norm_gain: float32 [3584], replicated, may hold values from 0.5 to 1.5
- qkv_weight: bfloat16 [3584, 4608], P('fsdp'), may hold values from -0.09375 to 0.09375
- qkv_bias: float32 [4608], replicated, may hold values from -40 to 40
- out_weight: bfloat16 [3584, 3584], P(None, 'fsdp'), may hold values from -0.09375 to 0.09375
- final_gain: float32 [3584], replicated, may hold values from 0.5 to 1.5
- value_head: float32 [3584], replicated, may hold values from -0.09375 to 0.09375
Outputs:
- hidden: bfloat16 [32, 128, 3584], P(('fsdp', 'dp'))
- margins: float32 [32], P(('fsdp', 'dp'))
- loss: float32 [], replicated
Inputs may be any that keep to these rules, and one draw needn't show every extreme that they name: partner[partner[i]] = i and partner[i] != i.
All inputs are finite; a program needn't handle non-finite values.
Results may differ from a plain program's by a relative error of at most 0.013.
The roundings to bfloat16 on the way count: a program that leaves them out, or rounds other values in their place, can miss the bound.
Values may be sent and summed in bfloat16 or wider, within the bound.
A program may use at most 128 MiB of HBM per device.

v0:
```python
import jax
import jax.numpy as jnp
from jax import lax
from jax.sharding import PartitionSpec as P

QUERY_HEADS = 28
KEY_VALUE_HEADS = 4
HEAD_SIZE = 128
QUERY_FEATURES = 3584
KEY_FEATURES = 512


def rms_scale(value_rows, gain):
    return (
        value_rows
        * lax.rsqrt(jnp.mean(value_rows * value_rows, axis=-1, keepdims=True) + 1e-06)
        * gain
    )


def apply_rotary(heads, length_rows):
    half = HEAD_SIZE // 2
    positions = jnp.arange(length_rows, dtype=jnp.float32)
    freqs = jnp.exp(
        -(2.0 * jnp.arange(half, dtype=jnp.float32) / HEAD_SIZE) * jnp.log(jnp.float32(1000000.0))
    )
    angles = positions[:, None] * freqs[None, :]
    cosine = jnp.cos(angles)
    sine = jnp.sin(angles)
    first = heads[..., :half]
    second = heads[..., half:]
    return jnp.concatenate(
        [first * cosine - second * sine, second * cosine + first * sine], axis=-1
    )


def attend(query_key_value, group_lengths, query_heads, key_value_heads):
    seq_count, length_rows, _ = query_key_value.shape
    query_width = query_heads * HEAD_SIZE
    key_width = key_value_heads * HEAD_SIZE
    query_rows = (
        query_key_value[..., :query_width]
        .reshape(seq_count, length_rows, query_heads, HEAD_SIZE)
        .transpose(0, 2, 1, 3)
    )
    key_rows = (
        query_key_value[..., query_width : query_width + key_width]
        .reshape(seq_count, length_rows, key_value_heads, HEAD_SIZE)
        .transpose(0, 2, 1, 3)
    )
    value_rows = (
        query_key_value[..., query_width + key_width :]
        .reshape(seq_count, length_rows, key_value_heads, HEAD_SIZE)
        .transpose(0, 2, 1, 3)
        .astype(jnp.bfloat16)
    )
    query_rows = (
        apply_rotary(query_rows, length_rows)
        .astype(jnp.bfloat16)
        .reshape(seq_count, key_value_heads, query_heads // key_value_heads, length_rows, HEAD_SIZE)
    )
    key_rows = apply_rotary(key_rows, length_rows).astype(jnp.bfloat16)
    scores = jnp.einsum(
        "bgqtd,bgsd->bgqts", query_rows, key_rows, preferred_element_type=jnp.float32
    ) / jnp.sqrt(jnp.float32(HEAD_SIZE))
    places = jnp.arange(length_rows, dtype=jnp.int32)
    causal = places[None, :] <= places[:, None]
    usable = places[None, :] < group_lengths[:, None]
    allowed = causal[None, :, :] & usable[:, None, :]
    scores = jnp.where(allowed[:, None, None, :, :], scores, jnp.float32(-1e30))
    highest = jnp.max(scores, axis=-1, keepdims=True)
    expd = jnp.exp(scores - highest)
    probs = (expd / jnp.sum(expd, axis=-1, keepdims=True)).astype(jnp.bfloat16)
    mixed = jnp.einsum("bgqts,bgsd->bgqtd", probs, value_rows, preferred_element_type=jnp.float32)
    mixed = mixed.reshape(seq_count, query_heads, length_rows, HEAD_SIZE).transpose(0, 2, 1, 3)
    return mixed.reshape(seq_count * length_rows, query_width).astype(jnp.bfloat16)


def per_device(
    tokens,
    lengths,
    partner,
    pair_weight,
    norm_gain,
    qkv_weight,
    qkv_bias,
    out_weight,
    final_gain,
    value_head,
):
    sequence = tokens[0]
    length = lengths[0]
    length_rows = sequence.shape[0]
    width = sequence.shape[1]
    normed = rms_scale(sequence.astype(jnp.float32), norm_gain).astype(jnp.bfloat16)
    query_group_count = lax.axis_size("dp")
    group_index = lax.axis_index("dp")
    query_heads = QUERY_HEADS // query_group_count
    key_value_heads = KEY_VALUE_HEADS // query_group_count
    query_cols = query_heads * HEAD_SIZE
    key_cols = key_value_heads * HEAD_SIZE
    group_normed, group_lengths = (
        lax.all_gather(normed[None], "dp", axis=0, tiled=True),
        lax.all_gather(lengths, "dp", axis=0, tiled=True),
    )
    seq_count = group_normed.shape[0]
    flat = group_normed.reshape(seq_count * length_rows, width)
    qkv_cols = jnp.concatenate(
        [
            lax.dynamic_slice_in_dim(qkv_weight, group_index * query_cols, query_cols, 1),
            lax.dynamic_slice_in_dim(
                qkv_weight, QUERY_FEATURES + group_index * key_cols, key_cols, 1
            ),
            lax.dynamic_slice_in_dim(
                qkv_weight, QUERY_FEATURES + KEY_FEATURES + group_index * key_cols, key_cols, 1
            ),
        ],
        axis=1,
    )
    bias_cols = jnp.concatenate(
        [
            lax.dynamic_slice_in_dim(qkv_bias, group_index * query_cols, query_cols, 0),
            lax.dynamic_slice_in_dim(
                qkv_bias, QUERY_FEATURES + group_index * key_cols, key_cols, 0
            ),
            lax.dynamic_slice_in_dim(
                qkv_bias, QUERY_FEATURES + KEY_FEATURES + group_index * key_cols, key_cols, 0
            ),
        ],
        axis=0,
    )
    out_rows = lax.dynamic_slice_in_dim(out_weight, group_index * query_cols, query_cols, 0)
    qkv_full, out_full = (
        lax.all_gather(qkv_cols, "fsdp", axis=0, tiled=True),
        lax.all_gather(out_rows, "fsdp", axis=1, tiled=True),
    )
    query_key_value = jnp.dot(flat, qkv_full, preferred_element_type=jnp.float32) + bias_cols
    attn = attend(
        query_key_value.reshape(seq_count, length_rows, -1),
        group_lengths,
        query_heads,
        key_value_heads,
    )
    projected = lax.psum_scatter(
        jnp.dot(attn, out_full, preferred_element_type=jnp.float32),
        "dp",
        scatter_dimension=0,
        tiled=True,
    )
    hidden = (sequence.astype(jnp.float32) + projected).astype(jnp.bfloat16)
    last = lax.dynamic_slice_in_dim(hidden, length - 1, 1, 0)[0].astype(jnp.float32)
    score = jnp.sum(rms_scale(last, final_gain) * value_head)
    everyone, weights_all = (
        lax.all_gather(score.reshape(1), ("fsdp", "dp"), axis=0, tiled=True),
        lax.all_gather(pair_weight, ("fsdp", "dp"), axis=0, tiled=True),
    )
    total_seqs = everyone.shape[0]
    mine = lax.axis_index(("fsdp", "dp"))
    index_all = jnp.arange(total_seqs, dtype=jnp.int32)
    my_partner = jnp.sum(jnp.where(index_all == mine, partner, 0))
    other = jnp.sum(jnp.where(index_all == my_partner, everyone, jnp.float32(0.0)))
    margin = jnp.where(mine < my_partner, score - other, other - score)
    matches = partner[:, None] == index_all[None, :]
    others_all = jnp.sum(jnp.where(matches, everyone[None, :], jnp.float32(0.0)), axis=1)
    margins_all = jnp.where(index_all < partner, everyone - others_all, others_all - everyone)
    loss = jnp.sum(weights_all * jax.nn.softplus(-margins_all)) / total_seqs
    return (hidden[None], margin.reshape(1), loss)


def solution(mesh):
    return jax.shard_map(
        per_device,
        mesh=mesh,
        in_specs=(
            P(("fsdp", "dp"), None, None),
            P(("fsdp", "dp")),
            P(),
            P(("fsdp", "dp")),
            P(),
            P("fsdp", None),
            P(),
            P(None, "fsdp"),
            P(),
            P(),
        ),
        out_specs=(P(("fsdp", "dp"), None, None), P(("fsdp", "dp")), P()),
        check_vma=False,
    )
```

profile of v0, /device:TPU:0, one launch (start us, length us, event | category | flops | bytes accessed | tf_op | source)
XLA Modules:
  0.0 405.5 jit_solution(7557553323519974288)
XLA Ops:
  7.2 1.6 fusion.3
  8.8 2.4 fusion.6
  11.3 1.0 constant_dynamic-slice_fusion.2
  12.3 1.2 constant_dynamic-slice_fusion.3
  13.5 1.0 pad_maximum_fusion
  14.6 1.0 constant_dynamic-slice_fusion
  17.7 6.4 %all-reduce = s32[4]{0:T(128)S(1)} all-reduce(s32[4]{0:T(128)S(1)} %dynamic-update-slice), channel_id=1, replica_groups=mesh['fsdp'=8,'dp'=4] {'dp'}, use_global_device_ids=true, to_apply=%add | all-reduce | flops 4 | bytes 32
  26.1 19.5 %all-gather.4.cloned.1.call-done = bf16[4,128,3584]{2,1,0:T(8,128)(2,1)} async-done(((bf16[1,128,3584]{2,1,0:T(8,128)(2,1)}), bf16[4,128,3584]{2,1,0:T(8,128)(2,1)}) %all-gather.4.cloned.1.call-update) | async-done | bytes 3670032 | tf_op jit(solution)/shard_map/all_gather | solution.py:103
  45.6 125.1 %all-gather.6.cloned.1.call-done = bf16[3584,1152]{1,0:T(8,128)(2,1)} async-done(((bf16[448,1152]{1,0:T(8,128)(2,1)}), bf16[3584,1152]{1,0:T(8,128)(2,1)}) %all-gather.6.cloned.1.call-update) | async-done | bytes 8257552 | tf_op jit(solution)/shard_map/all_gather | solution.py:134
  170.7 9.4 %convolution_add_fusion = f32[512,1152]{1,0:T(8,128)S(1)} fusion(bf16[512,3584]{1,0:T(8,128)(2,1)} %bitcast.61, bf16[3584,1152]{1,0:T(8,128)(2,1)} %all-gather.6.cloned.1.call-done, f32[1152]{0:T(1024)S(1)} %pad_maximum_fusion.1), kind=kOutput, calls=%fused_computation.1 | convolution fusion | flops 4228448256 | bytes 14291456 | tf_op jit(solution)/shard_map/dot_general | solution.py:137
  180.0 1.4 copy-done.1
  181.5 1.3 slice.29
  182.8 2.7 copy.23
  185.5 2.7 copy.24
  190.1 4.0 subtract_convert_fusion
  194.1 3.8 fusion.42
  197.8 2.9 fusion.8
  200.8 2.3 copy.26
  203.1 68.2 %all-gather.8.cloned.1.call-done = bf16[896,3584]{0,1:T(8,128)(2,1)} async-done(((bf16[896,448]{0,1:T(8,128)(2,1)}), bf16[896,3584]{0,1:T(8,128)(2,1)}) %all-gather.8.cloned.1.call-update) | async-done | bytes 6422544 | tf_op jit(solution)/shard_map/all_gather | solution.py:135
  271.3 10.1 %fusion.9 = f32[512,3584]{1,0:T(8,128)} fusion(bf16[896,3584]{0,1:T(8,128)(2,1)} %all-gather.8.cloned.1.call-done, bf16[112,8,4,128]{3,2,1,0:T(4,128)(2,1)} %bitcast.60), kind=kOutput, calls=%fused_computation.19 | convolution fusion | flops 3288334336 | bytes 14680064 | tf_op jit(solution)/shard_map/dot_general | solution.py:145
  282.8 62.9 %reduce-scatter.2.cloned.1.call-done = f32[128,3584]{1,0:T(8,128)} async-done(((f32[512,3584]{1,0:T(8,128)}), f32[128,3584]{1,0:T(8,128)}) %reduce-scatter.2.cloned.1.call-update) | async-done | bytes 1835024 | tf_op jit(solution)/shard_map/reduce_scatter | solution.py:144
  345.7 1.9 fusion.4
  352.8 39.3 %all-reduce.3 = (f32[32]{0:T(128)S(1)}, f32[32]{0:T(128)S(1)}) all-reduce(f32[32]{0:T(128)S(1)} %dynamic-update-slice.2, f32[32]{0:T(128)S(1)} %dynamic-update-slice.1), channel_id=1, replica_groups=mesh['fsdp'=8,'dp'=4] {'fsdp','dp'}, use_global_device_ids=true, to_apply=%add.2 | all-reduce | flops 64 | bytes 512
  392.2 1.4 fusion.35
  (44 shorter events, 10.1 us)
Async XLA Ops:
  7.2 7.5 %copy-start = (bf16[3584,448]{0,1:T(8,128)(2,1)S(1)}, bf16[3584,448]{0,1:T(8,128)(2,1)}, u32[]{:S(2)}) copy-start(bf16[3584,448]{0,1:T(8,128)(2,1)} %param.17) | copy-start | bytes 9633796
  7.2 38.4 %all-gather.4.cloned.1.call-start = ((), (), s32[]{:S(2)}) async-start(), calls=%async_computation.1 | async-start | bytes 4587520 | tf_op jit(solution)/shard_map/all_gather | solution.py:103
  11.2 159.4 %all-gather.6.cloned.1.call-start = ((), (), s32[]{:S(2)}) async-start(), calls=%async_computation.2 | async-start | bytes 9289728 | tf_op jit(solution)/shard_map/all_gather | solution.py:134
  14.6 1.8 copy-start.6
  14.6 256.7 %all-gather.8.cloned.1.call-start = ((), (), s32[]{:S(2)}) async-start(), calls=%async_computation.3 | async-start | bytes 7225344 | tf_op jit(solution)/shard_map/all_gather | solution.py:135
  15.6 330.1 %reduce-scatter.2.cloned.1.call-start = ((), (), s32[]{:S(2)}) async-start(), calls=%async_computation.4 | async-start | bytes 9175040 | tf_op jit(solution)/shard_map/reduce_scatter | solution.py:144
  180.0 1.4 copy-start.1
  281.4 0.8 copy-start.5
  282.8 67.9 %copy-start.3 = (f32[3584]{0:T(1024)S(1)}, f32[3584]{0:T(1024)}, u32[]{:S(2)}) copy-start(f32[3584]{0:T(1024)} %param.19) | copy-start | bytes 43012
  282.8 67.9 %copy-start.4 = (f32[3584]{0:T(1024)S(1)}, f32[3584]{0:T(1024)}, u32[]{:S(2)}) copy-start(f32[3584]{0:T(1024)} %param.18) | copy-start | bytes 43012
  347.6 0.9 copy-start.2
Sparse Core Ops, SparseCore 0:
  11.4 34.1 all-gather.3
  47.8 122.8 all-gather.5
  172.9 98.3 all-gather.7
  281.5 64.1 reduce-scatter.1
where the time goes:
time: 406 us; the launch traced here: 405 us
  waiting for transfers between devices  276 us (68%)
  blocking collectives  45.7 us (11%)
  matrix products  26.2 us (6%)
  between operations  21.9 us (5%)
  local copies, waits for them, and re-layouts  19.4 us (5%)
  other arithmetic  16.5 us (4%)
    all_gather x1, waiting for transfers between devices, per_device(): lax.all_gather(qkv_cols, 'fsdp', axis=0, tiled=True)  125 us
    all_gather x1, waiting for transfers between devices, per_device(): lax.all_gather(out_rows, 'fsdp', axis=1, tiled=True)  68.2 us
    reduce_scatter x1, waiting for transfers between devices, per_device(): lax.psum_scatter(jnp.dot(attn, out_full, preferred_element_type=jnp.float...  62.9 us
    unnamed x2, blocking collectives  45.7 us
    all_gather x1, waiting for transfers between devices, per_device(): lax.all_gather(normed[None], 'dp', axis=0, tiled=True)  19.5 us
    dot_general x1, matrix products, per_device(): jnp.dot(attn, out_full, preferred_element_type=jnp.float32)  10.1 us
    dot_general x1, matrix products, per_device(): jnp.dot(flat, qkv_full, preferred_element_type=jnp.float32) + bias_cols  9.36 us
  transfers between devices with their start and end apart: 4, of which 4 were waited for; matrix products, arithmetic and copies ran while one was open for 10% of the time, Pallas kernels for 0%

commit v1 on v0

--- a/solution.py
+++ b/solution.py
@@ -1,6 +1,11 @@
+import functools
+
 import jax
 import jax.numpy as jnp
+import numpy as np
 from jax import lax
+from jax.experimental import pallas as pl
+from jax.experimental.pallas import tpu as pltpu
 from jax.sharding import PartitionSpec as P
 
 QUERY_HEADS = 28
@@ -76,6 +81,509 @@
     return mixed.reshape(seq_count * length_rows, query_width).astype(jnp.bfloat16)
 
 
+UP, DOWN, ACROSS = 0, 1, 2
+
+
+def rotary_tables(length_rows):
+    half = HEAD_SIZE // 2
+    freqs = 1000000.0 ** (-2.0 * np.arange(half) / HEAD_SIZE)
+    angles = np.arange(length_rows)[:, None] * freqs[None, :]
+    cosine, sine = np.cos(angles), np.sin(angles)
+    return (
+        np.concatenate([cosine, cosine], axis=1).astype(np.float32),
+        np.concatenate([-sine, sine], axis=1).astype(np.float32),
+    )
+
+
+def layer_kernel(
+    shards,
+    groups,
+    tokens,
+    qkv_weight,
+    out_weight,
+    lengths_tile,
+    norm_gain,
+    qkv_bias,
+    cosine,
+    sine,
+    summed,
+    qkv_full,
+    out_full,
+    tok_all,
+    len_all,
+    normed,
+    qkv_rows,
+    attn,
+    own,
+    part_out,
+    part_in,
+    local_sem,
+    recv_sem,
+    send_sem,
+    tok_send,
+    tok_recv,
+    len_send,
+    len_recv,
+    part_send,
+    part_recv,
+):
+    line = shards // 2
+    f = lax.axis_index("fsdp")
+    g = lax.axis_index("dp")
+    z = f // 2
+    y = f % 2
+    even = z % 2 == 0
+    seq_rows = tokens.shape[0]
+    depth = qkv_weight.shape[0]
+    width = tok_all.shape[2]
+    query_cols = QUERY_FEATURES // groups
+    key_cols = KEY_FEATURES // groups
+    heads = query_cols // HEAD_SIZE
+    half_depth = depth // 2
+    half_out = query_cols // 2
+    has_up = z < line - 1
+    has_down = z > 0
+
+    def slot(m, c, s):
+        if m == 0:
+            return qkv_full.at[pl.ds(pl.multiple_of(s * depth + c * half_depth, 32), half_depth)]
+        return out_full.at[s, pl.ds(c * half_out, half_out)]
+
+    locals_ = [[[], []], [[], []]]
+    count = 0
+    for c in range(2):
+        rows = pl.ds(c * half_depth, half_depth)
+        there = slot(0, c, f)
+        for start, size, to in (
+            (g * query_cols, query_cols, 0),
+            (QUERY_FEATURES + g * key_cols, key_cols, query_cols),
+            (QUERY_FEATURES + KEY_FEATURES + g * key_cols, key_cols, query_cols + key_cols),
+        ):
+            locals_[0][c].append(
+                pltpu.make_async_copy(
+                    qkv_weight.at[rows, pl.ds(pl.multiple_of(start, 128), size)],
+                    there.at[:, pl.ds(to, size)],
+                    local_sem.at[count],
+                )
+            )
+            count += 1
+    for c in range(2):
+        locals_[1][c].append(
+            pltpu.make_async_copy(
+                out_weight.at[pl.ds(pl.multiple_of(g * query_cols + c * half_out, 32), half_out)],
+                slot(1, c, f),
+                local_sem.at[count],
+            )
+        )
+        count += 1
+    tok_local = pltpu.make_async_copy(tokens, tok_all.at[g], local_sem.at[count])
+    len_local = pltpu.make_async_copy(lengths_tile, len_all.at[g], local_sem.at[count + 1])
+    for m in range(2):
+        for c in range(2):
+            for copy in locals_[m][c]:
+                copy.start()
+    tok_local.start()
+    len_local.start()
+
+    barrier = pltpu.get_barrier_semaphore()
+    across = 2 * z + 1 - y
+    pl.semaphore_signal(barrier, inc=1, device_id={"fsdp": across})
+
+    @pl.when(has_up)
+    def _():
+        pl.semaphore_signal(barrier, inc=1, device_id={"fsdp": f + 2})
+
+    @pl.when(has_down)
+    def _():
+        pl.semaphore_signal(barrier, inc=1, device_id={"fsdp": f - 2})
+
+    peers = [lax.rem(g + i, groups) for i in range(1, groups)]
+    for peer in peers:
+        pl.semaphore_signal(barrier, inc=1, device_id={"dp": peer})
+    pl.semaphore_wait(barrier, groups + has_up.astype(jnp.int32) + has_down.astype(jnp.int32))
+
+    started = []
+
+    def send(cond, way, m, c, s):
+        target = (f + 2, f - 2, across)[way]
+        copy = pltpu.make_async_remote_copy(
+            src_ref=slot(m, c, s),
+            dst_ref=slot(m, c, s),
+            send_sem=send_sem.at[way, m, c, s],
+            recv_sem=recv_sem.at[m, c, s],
+            device_id={"fsdp": target},
+        )
+        started.append((cond, copy))
+        if cond is None:
+            copy.start()
+        else:
+            pl.when(cond)(copy.start)
+
+    def arrived(m, c, s):
+        pltpu.make_async_copy(slot(m, c, s), slot(m, c, s), recv_sem.at[m, c, s]).wait()
+
+    def own_line(m, c):
+        send(has_up, UP, m, c, f)
+        send(has_down, DOWN, m, c, f)
+
+    def line_step(m, k):
+        for c in range(2):
+            below = z - k
+            above = z + k
+            s_below = 2 * jnp.maximum(below, 0) + y
+            s_above = 2 * jnp.minimum(above, line - 1) + y
+
+            @pl.when(below >= 0)
+            def _():
+                arrived(m, c, s_below)
+
+            send((below >= 0) & has_up, UP, m, c, s_below)
+            if k > 1 or c == 0:
+                send(below >= 0, ACROSS, m, c, s_below)
+            else:
+                send((below >= 0) & even, ACROSS, m, c, s_below)
+
+            @pl.when(above < line)
+            def _():
+                arrived(m, c, s_above)
+
+            send((above < line) & has_down, DOWN, m, c, s_above)
+            if k > 1 or c == 0:
+                send(above < line, ACROSS, m, c, s_above)
+            else:
+                send((above < line) & jnp.logical_not(even), ACROSS, m, c, s_above)
+
+    def half_step(m):
+        arrived(m, 1, across)
+        send(even, UP, m, 1, across)
+        send(jnp.logical_not(even), DOWN, m, 1, across)
+
+    for c in range(2):
+        for copy in locals_[0][c]:
+            copy.wait()
+        own_line(0, c)
+        send(None, ACROSS, 0, c, f)
+    small = []
+    for peer in peers:
+        for source, dest, ss, rs in (
+            (tokens, tok_all, tok_send, tok_recv),
+            (lengths_tile, len_all, len_send, len_recv),
+        ):
+            copy = pltpu.make_async_remote_copy(
+                src_ref=source,
+                dst_ref=dest.at[g],
+                send_sem=ss.at[peer],
+                recv_sem=rs.at[g],
+                device_id={"dp": peer},
+            )
+            copy.start()
+            small.append(copy)
+
+    line_step(0, 1)
+    for k in range(2, line - 1):
+        line_step(0, k)
+    half_step(0)
+    for c in range(2):
+        for copy in locals_[1][c]:
+            copy.wait()
+        own_line(1, c)
+
+    tok_local.wait()
+    len_local.wait()
+    for peer in peers:
+        pltpu.make_async_copy(tok_all.at[peer], tok_all.at[peer], tok_recv.at[peer]).wait()
+        pltpu.make_async_copy(len_all.at[peer], len_all.at[peer], len_recv.at[peer]).wait()
+
+    norm_rows = 16
+    for j in range(groups):
+
+        @pl.loop(0, seq_rows // norm_rows)
+        def _(i):
+            at = pl.multiple_of(i * norm_rows, norm_rows)
+            rows = tok_all[j, pl.ds(at, norm_rows), :].astype(jnp.float32)
+            scale = lax.rsqrt(jnp.mean(rows * rows, axis=-1, keepdims=True) + 1e-06)
+            normed[pl.ds(pl.multiple_of(j * seq_rows + at, norm_rows), norm_rows), :] = (
+                rows * scale * norm_gain[...]
+            ).astype(jnp.bfloat16)
+
+    line_step(0, line - 1)
+    for c in range(2):
+        send(None, ACROSS, 1, c, f)
+
+    def across_wait(m, k):
+        for c in range(2):
+            if k == 0:
+                if c == 0:
+                    arrived(m, c, across)
+                continue
+            for there, ok in ((z - k, z - k >= 0), (z + k, z + k < line)):
+                s = 2 * jnp.clip(there, 0, line - 1) + 1 - y
+
+                @pl.when(ok)
+                def _():
+                    arrived(m, c, s)
+
+    for k in range(line):
+        across_wait(0, k)
+
+    tile = 3 * HEAD_SIZE
+
+    @pl.loop(0, (query_cols + 2 * key_cols) // tile)
+    def _(t):
+        cols = pl.ds(pl.multiple_of(t * tile, tile), tile)
+        qkv_rows[:, cols] = jnp.dot(
+            normed[...], qkv_full[:, cols], preferred_element_type=jnp.float32
+        )
+
+    def head_rows(j, column, bias_at):
+        rows = qkv_rows[pl.ds(pl.multiple_of(j * seq_rows, seq_rows), seq_rows), pl.ds(column, HEAD_SIZE)]
+        return rows + qkv_bias[:, pl.ds(pl.multiple_of(bias_at, HEAD_SIZE), HEAD_SIZE)]
+
+    def rotate(rows):
+        return (
+            rows * cosine[...] + pltpu.roll(rows, HEAD_SIZE // 2, 1) * sine[...]
+        ).astype(jnp.bfloat16)
+
+    key_heads = key_cols // HEAD_SIZE
+    share = heads // key_heads
+
+    def attend_sequence(j):
+        query_place = lax.broadcasted_iota(jnp.int32, (seq_rows, seq_rows), 0)
+        key_place = lax.broadcasted_iota(jnp.int32, (seq_rows, seq_rows), 1)
+        allowed = (key_place <= query_place) & (key_place < len_all[j, 0:1, :])
+        at = pl.ds(pl.multiple_of(j * seq_rows, seq_rows), seq_rows)
+        for kh in range(key_heads):
+            offset = kh * HEAD_SIZE
+            key = rotate(
+                head_rows(j, query_cols + offset, QUERY_FEATURES + g * key_cols + offset)
+            )
+            value = head_rows(
+                j,
+                query_cols + key_cols + offset,
+                QUERY_FEATURES + KEY_FEATURES + g * key_cols + offset,
+            ).astype(jnp.bfloat16)
+            for h in range(kh * share, (kh + 1) * share):
+                query = rotate(head_rows(j, h * HEAD_SIZE, g * query_cols + h * HEAD_SIZE))
+                scores = lax.dot_general(
+                    query, key, (((1,), (1,)), ((), ())), preferred_element_type=jnp.float32
+                ) / np.float32(np.sqrt(HEAD_SIZE))
+                scores = jnp.where(allowed, scores, jnp.float32(-1e30))
+                expd = jnp.exp(scores - jnp.max(scores, axis=-1, keepdims=True))
+                probs = (expd / jnp.sum(expd, axis=-1, keepdims=True)).astype(jnp.bfloat16)
+                attn[at, h * HEAD_SIZE : (h + 1) * HEAD_SIZE] = jnp.dot(
+                    probs, value, preferred_element_type=jnp.float32
+                ).astype(jnp.bfloat16)
+
+    pl.loop(0, groups // 2)(attend_sequence)
+    line_step(1, 1)
+    pl.loop(groups // 2, groups)(attend_sequence)
+
+    def part_copy(peer, s):
+        return pltpu.make_async_remote_copy(
+            src_ref=part_out.at[s, pl.ds(pl.multiple_of(peer * seq_rows, seq_rows), seq_rows)],
+            dst_ref=part_in.at[g, s],
+            send_sem=part_send.at[peer, s],
+            recv_sem=part_recv.at[g, s],
+            device_id={"dp": peer},
+        )
+
+    def project(s):
+        result = jnp.dot(attn[...], out_full[s], preferred_element_type=jnp.float32)
+        part_out[s] = result.astype(jnp.bfloat16)
+        for j in range(groups):
+
+            @pl.when(g == j)
+            def _():
+                own[s] = result[j * seq_rows : (j + 1) * seq_rows]
+
+        for peer in peers:
+            part_copy(peer, s).start()
+
+    def project_places(k, side):
+        @pl.loop(0, 1 if k == 0 else 2)
+        def _(i):
+            there = z + (2 * i - 1) * k
+
+            @pl.when((there >= 0) & (there < line))
+            def _():
+                project(2 * there + side)
+
+    for k in range(2, line - 1):
+        line_step(1, k)
+    half_step(1)
+    across_wait(1, 0)
+
+    @pl.loop(0, 2)
+    def _(side):
+        project(2 * z + side)
+
+    project_places(1, y)
+    line_step(1, line - 1)
+    for k in range(2, line):
+        project_places(k, y)
+    for k in range(1, line):
+        across_wait(1, k)
+        project_places(k, 1 - y)
+
+    @pl.loop(0, shards)
+    def _(s):
+        total = own[s]
+        for peer in peers:
+            pltpu.make_async_copy(
+                part_in.at[peer, s], part_in.at[peer, s], part_recv.at[peer, s]
+            ).wait()
+            total += part_in[peer, s].astype(jnp.float32)
+        summed[s] = total
+
+    for cond, copy in started:
+        if cond is None:
+            copy.wait_send()
+        else:
+            pl.when(cond)(copy.wait_send)
+    for copy in small:
+        copy.wait_send()
+
+    @pl.loop(0, shards)
+    def _(s):
+        for peer in peers:
+            part_copy(peer, s).wait_send()
+
+
+def layer_fits(shards, groups, tokens, qkv_weight, out_weight):
+    return (
+        shards % 4 == 0
+        and shards >= 8
+        and qkv_weight.shape[0] % 32 == 0
+        and KEY_VALUE_HEADS % groups == 0
+        and tokens.shape[1] == HEAD_SIZE
+        and groups % 2 == 0
+    )
+
+
+def layer(tokens, lengths, norm_gain, qkv_weight, qkv_bias, out_weight):
+    shards, groups = lax.axis_size("fsdp"), lax.axis_size("dp")
+    _, seq_rows, width = tokens.shape
+    depth = qkv_weight.shape[0]
+    out_cols = out_weight.shape[1]
+    query_cols = QUERY_FEATURES // groups
+    key_cols = KEY_FEATURES // groups
+    all_cols = query_cols + 2 * key_cols
+    rows = groups * seq_rows
+    cosine, sine = rotary_tables(seq_rows)
+    lengths_tile = jnp.broadcast_to(lengths[:, None], (8, seq_rows))
+    dma = pltpu.SemaphoreType.DMA
+    vmem = pl.BlockSpec(memory_space=pltpu.VMEM)
+    anywhere = pl.BlockSpec(memory_space=pl.ANY)
+    bf16, f32 = jnp.bfloat16, jnp.float32
+    return pl.pallas_call(
+        functools.partial(layer_kernel, shards, groups),
+        out_shape=jax.ShapeDtypeStruct((shards, seq_rows, out_cols), f32),
+        in_specs=[anywhere, anywhere, anywhere, vmem, vmem, vmem, vmem, vmem],
+        out_specs=vmem,
+        scratch_shapes=[
+            pltpu.VMEM((shards * depth, all_cols), bf16),
+            pltpu.VMEM((shards, query_cols, out_cols), bf16),
+            pltpu.VMEM((groups, seq_rows, width), bf16),
+            pltpu.VMEM((groups, 8, seq_rows), jnp.int32),
+            pltpu.VMEM((rows, width), bf16),
+            pltpu.VMEM((rows, all_cols), f32),
+            pltpu.VMEM((rows, query_cols), bf16),
+            pltpu.VMEM((shards, seq_rows, out_cols), f32),
+            pltpu.VMEM((shards, rows, out_cols), bf16),
+            pltpu.VMEM((groups, shards, seq_rows, out_cols), bf16),
+            dma((10,)),
+            dma((2, 2, shards)),
+            dma((3, 2, 2, shards)),
+            dma((groups,)),
+            dma((groups,)),
+            dma((groups,)),
+            dma((groups,)),
+            dma((groups, shards)),
+            dma((groups, shards)),
+        ],
+        compiler_params=pltpu.CompilerParams(
+            collective_id=0, has_side_effects=True, vmem_limit_bytes=60 * 1024 * 1024
+        ),
+    )(
+        tokens[0],
+        qkv_weight,
+        out_weight,
+        lengths_tile,
+        norm_gain[None],
+        qkv_bias[None],
+        jnp.asarray(cosine),
+        jnp.asarray(sine),
+    )
+
+
+def projected_by_gathers(
+    tokens,
+    lengths,
+    norm_gain,
+    qkv_weight,
+    qkv_bias,
+    out_weight,
+):
+    sequence = tokens[0]
+    length_rows = sequence.shape[0]
+    width = sequence.shape[1]
+    normed = rms_scale(sequence.astype(jnp.float32), norm_gain).astype(jnp.bfloat16)
+    query_group_count = lax.axis_size("dp")
+    group_index = lax.axis_index("dp")
+    query_heads = QUERY_HEADS // query_group_count
+    key_value_heads = KEY_VALUE_HEADS // query_group_count
+    query_cols = query_heads * HEAD_SIZE
+    key_cols = key_value_heads * HEAD_SIZE
+    group_normed, group_lengths = (
+        lax.all_gather(normed[None], "dp", axis=0, tiled=True),
+        lax.all_gather(lengths, "dp", axis=0, tiled=True),
+    )
+    seq_count = group_normed.shape[0]
+    flat = group_normed.reshape(seq_count * length_rows, width)
+    qkv_cols = jnp.concatenate(
+        [
+            lax.dynamic_slice_in_dim(qkv_weight, group_index * query_cols, query_cols, 1),
+            lax.dynamic_slice_in_dim(
+                qkv_weight, QUERY_FEATURES + group_index * key_cols, key_cols, 1
+            ),
+            lax.dynamic_slice_in_dim(
+                qkv_weight, QUERY_FEATURES + KEY_FEATURES + group_index * key_cols, key_cols, 1
+            ),
+        ],
+        axis=1,
+    )
+    bias_cols = jnp.concatenate(
+        [
+            lax.dynamic_slice_in_dim(qkv_bias, group_index * query_cols, query_cols, 0),
+            lax.dynamic_slice_in_dim(
+                qkv_bias, QUERY_FEATURES + group_index * key_cols, key_cols, 0
+            ),
+            lax.dynamic_slice_in_dim(
+                qkv_bias, QUERY_FEATURES + KEY_FEATURES + group_index * key_cols, key_cols, 0
+            ),
+        ],
+        axis=0,
+    )
+    out_rows = lax.dynamic_slice_in_dim(out_weight, group_index * query_cols, query_cols, 0)
+    qkv_full, out_full = (
+        lax.all_gather(qkv_cols, "fsdp", axis=0, tiled=True),
+        lax.all_gather(out_rows, "fsdp", axis=1, tiled=True),
+    )
+    query_key_value = jnp.dot(flat, qkv_full, preferred_element_type=jnp.float32) + bias_cols
+    attn = attend(
+        query_key_value.reshape(seq_count, length_rows, -1),
+        group_lengths,
+        query_heads,
+        key_value_heads,
+    )
+    return lax.psum_scatter(
+        jnp.dot(attn, out_full, preferred_element_type=jnp.float32),
+        "dp",
+        scatter_dimension=0,
+        tiled=True,
+    )
+
+
 def per_device(
     tokens,
     lengths,
@@ -90,63 +598,11 @@
 ):
     sequence = tokens[0]
     length = lengths[0]
-    length_rows = sequence.shape[0]
-    width = sequence.shape[1]
-    normed = rms_scale(sequence.astype(jnp.float32), norm_gain).astype(jnp.bfloat16)
-    query_group_count = lax.axis_size("dp")
-    group_index = lax.axis_index("dp")
-    query_heads = QUERY_HEADS // query_group_count
-    key_value_heads = KEY_VALUE_HEADS // query_group_count
-    query_cols = query_heads * HEAD_SIZE
-    key_cols = key_value_heads * HEAD_SIZE
-    group_normed, group_lengths = (
-        lax.all_gather(normed[None], "dp", axis=0, tiled=True),
-        lax.all_gather(lengths, "dp", axis=0, tiled=True),
-    )
-    seq_count = group_normed.shape[0]
-    flat = group_normed.reshape(seq_count * length_rows, width)
-    qkv_cols = jnp.concatenate(
-        [
-            lax.dynamic_slice_in_dim(qkv_weight, group_index * query_cols, query_cols, 1),
-            lax.dynamic_slice_in_dim(
-                qkv_weight, QUERY_FEATURES + group_index * key_cols, key_cols, 1
-            ),
-            lax.dynamic_slice_in_dim(
-                qkv_weight, QUERY_FEATURES + KEY_FEATURES + group_index * key_cols, key_cols, 1
-            ),
-        ],
-        axis=1,
-    )
-    bias_cols = jnp.concatenate(
-        [
-            lax.dynamic_slice_in_dim(qkv_bias, group_index * query_cols, query_cols, 0),
-            lax.dynamic_slice_in_dim(
-                qkv_bias, QUERY_FEATURES + group_index * key_cols, key_cols, 0
-            ),
-            lax.dynamic_slice_in_dim(
-                qkv_bias, QUERY_FEATURES + KEY_FEATURES + group_index * key_cols, key_cols, 0
-            ),
-        ],
-        axis=0,
-    )
-    out_rows = lax.dynamic_slice_in_dim(out_weight, group_index * query_cols, query_cols, 0)
-    qkv_full, out_full = (
-        lax.all_gather(qkv_cols, "fsdp", axis=0, tiled=True),
-        lax.all_gather(out_rows, "fsdp", axis=1, tiled=True),
-    )
-    query_key_value = jnp.dot(flat, qkv_full, preferred_element_type=jnp.float32) + bias_cols
-    attn = attend(
-        query_key_value.reshape(seq_count, length_rows, -1),
-        group_lengths,
-        query_heads,
-        key_value_heads,
-    )
-    projected = lax.psum_scatter(
-        jnp.dot(attn, out_full, preferred_element_type=jnp.float32),
-        "dp",
-        scatter_dimension=0,
-        tiled=True,
-    )
+    args = (tokens, lengths, norm_gain, qkv_weight, qkv_bias, out_weight)
+    if layer_fits(lax.axis_size("fsdp"), lax.axis_size("dp"), tokens, qkv_weight, out_weight):
+        projected = layer(*args).transpose(1, 0, 2).reshape(sequence.shape)
+    else:
+        projected = projected_by_gathers(*args)
     hidden = (sequence.astype(jnp.float32) + projected).astype(jnp.bfloat16)
     last = lax.dynamic_slice_in_dim(hidden, length - 1, 1, 0)[0].astype(jnp.float32)
     score = jnp.sum(rms_scale(last, final_gain) * value_head)

time: 406 us -> 246 us (0.61)
  waiting for transfers between devices: 276 us -> 0 us
  Pallas kernels: 0 us -> 175 us
  matrix products: 26.2 us -> 0 us
  between operations: 21.9 us -> 8.93 us
  other arithmetic: 16.5 us -> 5.05 us
  blocking collectives: 45.7 us -> 39.3 us
    all_gather x3 -> x0, waiting for transfers between devices: 213 us -> none  [the longest x1 125 us: per_device(): lax.all_gather(qkv_cols, 'fsdp', axis=0, tiled=True)]
    pallas_call x0 -> x1, Pallas kernels: none -> 175 us  [layer(): pl.pallas_call(functools.partial(layer_kernel, shards, groups), out_shape...]
    reduce_scatter x1 -> x0, waiting for transfers between devices: 62.9 us -> none  [per_device(): lax.psum_scatter(jnp.dot(attn, out_full, preferred_element_type=jnp.float...]
    dot_general x3 -> x0, matrix products: 22.4 us -> none  [the longest x1 10.1 us: per_device(): jnp.dot(attn, out_full, preferred_element_type=jnp.float32)]
    unnamed x21 -> x20, local copies, waits for them, and re-layouts: 4.56 us -> 11.3 us
    unnamed x2 -> x1, blocking collectives: 45.7 us -> 39.3 us
    slice x2 -> x0, local copies, waits for them, and re-layouts: 4.09 us -> none  [attend(): query_key_value[..., :query_width]]
  transfers between devices with their start and end apart: 4 -> 0, of which waited for: 4 -> 0; matrix products, arithmetic and copies ran while one was open for 10% -> 0% of each run, Pallas kernels for 0% -> 0%
where the time goes in v1:
time: 246 us; the launch traced here: 245 us
  Pallas kernels  175 us (71%)
  blocking collectives  39.3 us (16%)
  local copies, waits for them, and re-layouts  16.8 us (7%)
  between operations  8.93 us (4%)
  other arithmetic  5.05 us (2%)
    pallas_call x1, Pallas kernels, layer(): pl.pallas_call(functools.partial(layer_kernel, shards, groups), out_shape...  175 us
    unnamed x1, blocking collectives  39.3 us
    unnamed x20, local copies, waits for them, and re-layouts  11.3 us

profile of v1, /device:TPU:0, one launch (start us, length us, event | category | flops | bytes accessed | tf_op | source)
XLA Modules:
  0.0 245.0 jit_solution(12981017207803051090)
XLA Ops:
  1.3 0.6 broadcast_in_dim.40.lengths_tile
  1.9 5.8 %copy.24.out_weight = bf16[3584,448]{1,0:T(8,128)(2,1)} copy(bf16[3584,448]{0,1:T(8,128)(2,1)} %param.19) | data formatting | bytes 6422528 | tf_op args[7]
  7.6 0.0 copy-done.1
  7.6 0.6 broadcast_in_dim.42.qkv_bias
  8.3 0.0 copy-done.4
  8.3 0.6 broadcast_in_dim.41.norm_gain
  8.9 174.8 %shard_map.139 = f32[8,128,448]{2,1,0:T(8,128)} custom-call(bf16[128,3584]{1,0:T(8,128)(2,1)} %bitcast.15, bf16[448,4608]{1,0:T(8,128)(2,1)} %qkv_weight.1, bf16[3584,448]{1,0:T(8,128)(2,1)} %copy.24.out_weight, s32[8,128]{1,0:T(8,128)} %broadcast_in_dim.40.lengths_tile, f32[1,3584]{1,0:T(1,128)} %broadcast_in_dim.41.norm_gain, ...), custom_call_target="tpu_custom_call" | custom-call | tf_op jit(solution)/shard_map/pallas_call | solution.py:478
  183.7 1.9 copy.25
  185.6 1.8 constant_dynamic-slice_fusion
  187.4 2.1 copy.29
  189.5 0.0 copy-done
  189.5 0.6 multiply_reduce_fusion.2
  190.9 0.1 multiply_reduce_fusion.1
  190.9 0.0 copy-done.2
  191.0 0.6 multiply_reduce_fusion
  191.6 0.8 dynamic-update-slice
  193.0 0.1 dynamic-update-slice.1
  193.1 39.3 %all-reduce.2 = (f32[32]{0:T(128)S(1)}, f32[32]{0:T(128)S(1)}) all-reduce(f32[32]{0:T(128)S(1)} %dynamic-update-slice.1, f32[32]{0:T(128)S(1)} %dynamic-update-slice), channel_id=1, replica_groups=mesh['fsdp'=8,'dp'=4] {'fsdp','dp'}, use_global_device_ids=true, to_apply=%add.1 | all-reduce | flops 64 | bytes 512
  232.4 0.2 select_reduce_fusion
  232.6 0.6 fusion.4
  233.2 1.3 fusion.8
  238.6 1.3 copy.23
  239.8 1.6 fusion
  241.4 1.3 copy.28
  (10 shorter events, 0.0 us)
Async XLA Ops:
  1.9 5.8 %copy-start.1 = (f32[4608]{0:T(1024)S(1)}, f32[4608]{0:T(1024)}, u32[]{:S(2)}) copy-start(f32[4608]{0:T(1024)} %param.18) | copy-start | bytes 55300
  1.9 6.4 %copy-start.4 = (f32[3584]{0:T(1024)S(1)}, f32[3584]{0:T(1024)}, u32[]{:S(2)}) copy-start(f32[3584]{0:T(1024)} %param.16) | copy-start | bytes 43012
  187.4 2.1 copy-start
  187.4 3.5 %copy-start.2 = (f32[3584]{0:T(1024)S(1)}, f32[3584]{0:T(1024)}, u32[]{:S(2)}) copy-start(f32[3584]{0:T(1024)} %param.21) | copy-start | bytes 43012
  187.4 3.6 %copy-start.3 = (f32[3584]{0:T(1024)S(1)}, f32[3584]{0:T(1024)}, u32[]{:S(2)}) copy-start(f32[3584]{0:T(1024)} %param.20) | copy-start | bytes 43012
  187.4 45.0 %copy-start.5 = (s32[32]{0:T(128)S(1)}, s32[32]{0:T(128)}, u32[]{:S(2)}) copy-start(s32[32]{0:T(128)} %param.14) | copy-start | bytes 388

commit v2 on v1

--- a/solution.py
+++ b/solution.py
@@ -101,15 +101,22 @@
     tokens,
     qkv_weight,
     out_weight,
-    lengths_tile,
+    length,
+    pair_weight,
+    partner,
     norm_gain,
+    final_gain,
+    value_head,
     qkv_bias,
     cosine,
     sine,
-    summed,
+    hidden,
+    margin_out,
+    loss_out,
     qkv_full,
     out_full,
     tok_all,
+    len_tile,
     len_all,
     normed,
     qkv_rows,
@@ -117,6 +124,9 @@
     own,
     part_out,
     part_in,
+    score_tile,
+    score_all,
+    partner_rows,
     local_sem,
     recv_sem,
     send_sem,
@@ -126,6 +136,8 @@
     len_recv,
     part_send,
     part_recv,
+    score_send,
+    score_recv,
 ):
     line = shards // 2
     f = lax.axis_index("fsdp")
@@ -140,7 +152,7 @@
     key_cols = KEY_FEATURES // groups
     heads = query_cols // HEAD_SIZE
     half_depth = depth // 2
-    half_out = query_cols // 2
+    half_out = out_weight.shape[0] // 2
     has_up = z < line - 1
     has_down = z > 0
 
@@ -170,37 +182,38 @@
     for c in range(2):
         locals_[1][c].append(
             pltpu.make_async_copy(
-                out_weight.at[pl.ds(pl.multiple_of(g * query_cols + c * half_out, 32), half_out)],
+                out_weight.at[
+                    pl.ds(c * half_out, half_out),
+                    pl.ds(pl.multiple_of(g * query_cols, 128), query_cols),
+                ],
                 slot(1, c, f),
                 local_sem.at[count],
             )
         )
         count += 1
     tok_local = pltpu.make_async_copy(tokens, tok_all.at[g], local_sem.at[count])
-    len_local = pltpu.make_async_copy(lengths_tile, len_all.at[g], local_sem.at[count + 1])
+    len_tile[...] = jnp.full(len_tile.shape, length[0], jnp.int32)
+    len_all[g] = len_tile[...]
     for m in range(2):
         for c in range(2):
             for copy in locals_[m][c]:
                 copy.start()
     tok_local.start()
-    len_local.start()
 
     barrier = pltpu.get_barrier_semaphore()
     across = 2 * z + 1 - y
-    pl.semaphore_signal(barrier, inc=1, device_id={"fsdp": across})
-
-    @pl.when(has_up)
-    def _():
-        pl.semaphore_signal(barrier, inc=1, device_id={"fsdp": f + 2})
-
-    @pl.when(has_down)
-    def _():
-        pl.semaphore_signal(barrier, inc=1, device_id={"fsdp": f - 2})
+    everyone = shards * groups
+    me = f * groups + g
+
+    @pl.loop(1, everyone)
+    def _(i):
+        other = lax.rem(me + i, everyone)
+        pl.semaphore_signal(
+            barrier, inc=1, device_id={"fsdp": other // groups, "dp": lax.rem(other, groups)}
+        )
 
     peers = [lax.rem(g + i, groups) for i in range(1, groups)]
-    for peer in peers:
-        pl.semaphore_signal(barrier, inc=1, device_id={"dp": peer})
-    pl.semaphore_wait(barrier, groups + has_up.astype(jnp.int32) + has_down.astype(jnp.int32))
+    pl.semaphore_wait(barrier, everyone - 1)
 
     started = []
 
@@ -267,7 +280,7 @@
     for peer in peers:
         for source, dest, ss, rs in (
             (tokens, tok_all, tok_send, tok_recv),
-            (lengths_tile, len_all, len_send, len_recv),
+            (len_tile, len_all, len_send, len_recv),
         ):
             copy = pltpu.make_async_remote_copy(
                 src_ref=source,
@@ -289,7 +302,6 @@
         own_line(1, c)
 
     tok_local.wait()
-    len_local.wait()
     for peer in peers:
         pltpu.make_async_copy(tok_all.at[peer], tok_all.at[peer], tok_recv.at[peer]).wait()
         pltpu.make_async_copy(len_all.at[peer], len_all.at[peer], len_recv.at[peer]).wait()
@@ -388,7 +400,12 @@
         )
 
     def project(s):
-        result = jnp.dot(attn[...], out_full[s], preferred_element_type=jnp.float32)
+        result = lax.dot_general(
+            attn[...],
+            out_full[s],
+            (((1,), (1,)), ((), ())),
+            preferred_element_type=jnp.float32,
+        )
         part_out[s] = result.astype(jnp.bfloat16)
         for j in range(groups):
 
@@ -427,13 +444,75 @@
 
     @pl.loop(0, shards)
     def _(s):
-        total = own[s]
         for peer in peers:
             pltpu.make_async_copy(
                 part_in.at[peer, s], part_in.at[peer, s], part_recv.at[peer, s]
             ).wait()
-            total += part_in[peer, s].astype(jnp.float32)
-        summed[s] = total
+
+    block = 32
+    out_cols = own.shape[2]
+
+    @pl.loop(0, seq_rows // block)
+    def _(i):
+        at = pl.ds(pl.multiple_of(i * block, block), block)
+        for p in range(shards // 2):
+            sums = []
+            for s in (2 * p, 2 * p + 1):
+                total = own[s, at]
+                for peer in peers:
+                    total += part_in[peer, s, at].astype(jnp.float32)
+                sums.append(total)
+            cols = slice(2 * p * out_cols, 2 * (p + 1) * out_cols)
+            hidden[at, cols] = (
+                tok_all[g, at, cols].astype(jnp.float32) + jnp.concatenate(sums, axis=1)
+            ).astype(jnp.bfloat16)
+
+    place = lax.broadcasted_iota(jnp.int32, len_tile.shape, 1)
+    pick = (place == len_tile[...] - 1).astype(jnp.bfloat16)
+    last = jnp.dot(pick, hidden[...], preferred_element_type=jnp.float32)
+    scale = lax.rsqrt(jnp.mean(last * last, axis=-1, keepdims=True) + 1e-06)
+    score = jnp.sum(last * scale * final_gain[...] * value_head[...], axis=-1, keepdims=True)
+    first_row = lax.broadcasted_iota(jnp.int32, score_tile.shape, 0) == 0
+    score_tile[...] = jnp.where(first_row, score, jnp.full(score_tile.shape, pair_weight[0]))
+    score_all[me] = score_tile[...]
+
+    def score_copy(i):
+        other = lax.rem(me + i, everyone)
+        return pltpu.make_async_remote_copy(
+            src_ref=score_tile,
+            dst_ref=score_all.at[me],
+            send_sem=score_send.at[other],
+            recv_sem=score_recv.at[me],
+            device_id={"fsdp": other // groups, "dp": lax.rem(other, groups)},
+        )
+
+    @pl.loop(1, everyone)
+    def _(i):
+        score_copy(i).start()
+
+    @pl.loop(0, everyone)
+    def _(i):
+        partner_rows[pl.ds(i, 1), :] = jnp.full((1, HEAD_SIZE), partner[i], jnp.int32)
+
+    @pl.loop(1, everyone)
+    def _(i):
+        other = lax.rem(me + i, everyone)
+        pltpu.make_async_copy(
+            score_all.at[other], score_all.at[other], score_recv.at[other]
+        ).wait()
+
+    scores = score_all[:, 0, :]
+    weights = score_all[:, 1, :]
+    row = lax.broadcasted_iota(jnp.int32, scores.shape, 0)
+    lane = lax.broadcasted_iota(jnp.int32, scores.shape, 1)
+    partners = partner_rows[...]
+    score_row = jnp.sum(jnp.where(row == lane, scores, 0.0), axis=0, keepdims=True)
+    others = jnp.sum(jnp.where(partners == lane, score_row, 0.0), axis=1, keepdims=True)
+    margins = jnp.where(row < partners, scores - others, others - scores)
+    softplus = jnp.maximum(-margins, 0.0) + jnp.log1p(jnp.exp(-jnp.abs(margins)))
+    first_lane = lane == 0
+    margin_out[0] = jnp.sum(jnp.where(first_lane & (row == me), margins, 0.0))
+    loss_out[0] = jnp.sum(jnp.where(first_lane, weights * softplus, 0.0)) / everyone
 
     for cond, copy in started:
         if cond is None:
@@ -447,6 +526,10 @@
     def _(s):
         for peer in peers:
             part_copy(peer, s).wait_send()
+
+    @pl.loop(1, everyone)
+    def _(i):
+        score_copy(i).wait_send()
 
 
 def layer_fits(shards, groups, tokens, qkv_weight, out_weight):
@@ -457,10 +540,23 @@
         and KEY_VALUE_HEADS % groups == 0
         and tokens.shape[1] == HEAD_SIZE
         and groups % 2 == 0
-    )
-
-
-def layer(tokens, lengths, norm_gain, qkv_weight, qkv_bias, out_weight):
+        and shards * groups <= HEAD_SIZE
+        and out_weight.shape[1] % 64 == 0
+    )
+
+
+def layer(
+    tokens,
+    lengths,
+    partner,
+    pair_weight,
+    norm_gain,
+    qkv_weight,
+    qkv_bias,
+    out_weight,
+    final_gain,
+    value_head,
+):
     shards, groups = lax.axis_size("fsdp"), lax.axis_size("dp")
     _, seq_rows, width = tokens.shape
     depth = qkv_weight.shape[0]
@@ -470,20 +566,26 @@
     all_cols = query_cols + 2 * key_cols
     rows = groups * seq_rows
     cosine, sine = rotary_tables(seq_rows)
-    lengths_tile = jnp.broadcast_to(lengths[:, None], (8, seq_rows))
+    everyone = shards * groups
     dma = pltpu.SemaphoreType.DMA
     vmem = pl.BlockSpec(memory_space=pltpu.VMEM)
     anywhere = pl.BlockSpec(memory_space=pl.ANY)
     bf16, f32 = jnp.bfloat16, jnp.float32
-    return pl.pallas_call(
+    scalar = pl.BlockSpec(memory_space=pltpu.SMEM)
+    hidden, margin, loss = pl.pallas_call(
         functools.partial(layer_kernel, shards, groups),
-        out_shape=jax.ShapeDtypeStruct((shards, seq_rows, out_cols), f32),
-        in_specs=[anywhere, anywhere, anywhere, vmem, vmem, vmem, vmem, vmem],
-        out_specs=vmem,
+        out_shape=(
+            jax.ShapeDtypeStruct((seq_rows, width), bf16),
+            jax.ShapeDtypeStruct((1,), f32),
+            jax.ShapeDtypeStruct((1,), f32),
+        ),
+        in_specs=[anywhere] * 3 + [scalar] * 3 + [vmem] * 6,
+        out_specs=(vmem, scalar, scalar),
         scratch_shapes=[
             pltpu.VMEM((shards * depth, all_cols), bf16),
-            pltpu.VMEM((shards, query_cols, out_cols), bf16),
+            pltpu.VMEM((shards, out_cols, query_cols), bf16),
             pltpu.VMEM((groups, seq_rows, width), bf16),
+            pltpu.VMEM((8, seq_rows), jnp.int32),
             pltpu.VMEM((groups, 8, seq_rows), jnp.int32),
             pltpu.VMEM((rows, width), bf16),
             pltpu.VMEM((rows, all_cols), f32),
@@ -491,6 +593,9 @@
             pltpu.VMEM((shards, seq_rows, out_cols), f32),
             pltpu.VMEM((shards, rows, out_cols), bf16),
             pltpu.VMEM((groups, shards, seq_rows, out_cols), bf16),
+            pltpu.VMEM((8, HEAD_SIZE), f32),
+            pltpu.VMEM((everyone, 8, HEAD_SIZE), f32),
+            pltpu.VMEM((everyone, HEAD_SIZE), jnp.int32),
             dma((10,)),
             dma((2, 2, shards)),
             dma((3, 2, 2, shards)),
@@ -500,6 +605,8 @@
             dma((groups,)),
             dma((groups, shards)),
             dma((groups, shards)),
+            dma((everyone,)),
+            dma((everyone,)),
         ],
         compiler_params=pltpu.CompilerParams(
             collective_id=0, has_side_effects=True, vmem_limit_bytes=60 * 1024 * 1024
@@ -507,13 +614,18 @@
     )(
         tokens[0],
         qkv_weight,
-        out_weight,
-        lengths_tile,
+        out_weight.T,
+        lengths,
+        pair_weight,
+        partner,
         norm_gain[None],
+        final_gain[None],
+        value_head[None],
         qkv_bias[None],
         jnp.asarray(cosine),
         jnp.asarray(sine),
     )
+    return hidden[None], margin, loss.reshape(())
 
 
 def projected_by_gathers(
@@ -596,13 +708,22 @@
     final_gain,
     value_head,
 ):
+    if layer_fits(lax.axis_size("fsdp"), lax.axis_size("dp"), tokens, qkv_weight, out_weight):
+        return layer(
+            tokens,
+            lengths,
+            partner,
+            pair_weight,
+            norm_gain,
+            qkv_weight,
+            qkv_bias,
+            out_weight,
+            final_gain,
+            value_head,
+        )
     sequence = tokens[0]
     length = lengths[0]
-    args = (tokens, lengths, norm_gain, qkv_weight, qkv_bias, out_weight)
-    if layer_fits(lax.axis_size("fsdp"), lax.axis_size("dp"), tokens, qkv_weight, out_weight):
-        projected = layer(*args).transpose(1, 0, 2).reshape(sequence.shape)
-    else:
-        projected = projected_by_gathers(*args)
+    projected = projected_by_gathers(tokens, lengths, norm_gain, qkv_weight, qkv_bias, out_weight)
     hidden = (sequence.astype(jnp.float32) + projected).astype(jnp.bfloat16)
     last = lax.dynamic_slice_in_dim(hidden, length - 1, 1, 0)[0].astype(jnp.float32)
     score = jnp.sum(rms_scale(last, final_gain) * value_head)

time: 246 us -> 191 us (0.78)
  blocking collectives: 39.3 us -> 0 us
  local copies, waits for them, and re-layouts: 16.8 us -> 7.48 us
  other arithmetic: 5.05 us -> 0 us
  between operations: 8.93 us -> 5.41 us
  Pallas kernels: 175 us -> 178 us
    unnamed x1 -> x0, blocking collectives: 39.3 us -> none
    unnamed x20 -> x1, local copies, waits for them, and re-layouts: 11.3 us -> 2.16 us
    reduce_sum x5 -> x0, other arithmetic: 3.41 us -> none  [the longest x1 1.35 us: per_device(): loss = jnp.sum(weights_all * jax.nn.softplus(-margins_all)) / total_seqs]
    pallas_call x1, Pallas kernels: 175 us -> 178 us  [layer(): pl.pallas_call(functools.partial(layer_kernel, shards, groups), out_shape...]
where the time goes in v2:
time: 191 us
  Pallas kernels  178 us (93%)
  local copies, waits for them, and re-layouts  7.48 us (4%)
  between operations  5.41 us (3%)
    pallas_call x1, Pallas kernels, layer(): pl.pallas_call(functools.partial(layer_kernel, shards, groups), out_shape...  178 us

profile of v2, /device:TPU:0, one launch (start us, length us, event | category | flops | bytes accessed | tf_op | source)
XLA Modules:
  0.0 190.9 jit_solution(14752931226058610379)
XLA Ops:
  1.9 1.3 broadcast_in_dim.15.norm_gain
  3.2 1.3 broadcast_in_dim.16.final_gain
  4.6 1.3 broadcast_in_dim.17.value_head
  5.9 1.3 broadcast_in_dim.18.qkv_bias
  7.2 178.1 %shard_map.139 = (bf16[128,3584]{1,0:T(8,128)(2,1)}, f32[1]{0:T(128)}, f32[1]{0:T(128)}) custom-call(bf16[128,3584]{1,0:T(8,128)(2,1)} %bitcast.5, bf16[448,4608]{1,0:T(8,128)(2,1)} %qkv_weight.1, bf16[448,3584]{1,0:T(8,128)(2,1)} %bitcast.4, s32[1]{0:T(128)S(6)} %copy.18.length, f32[1]{0:T(128)S(6)} %copy.19.pair_weight, s32[32]{0:T(128)} %partner.1, ...), custom_call_target="tpu_custom_call" | custom-call | tf_op jit(solution)/shard_map/pallas_call | solution.py:575
  185.3 2.2 %copy.20 = bf16[1,128,3584]{2,1,0:T(8,128)(2,1)} copy(bf16[1,128,3584]{2,1,0:T(8,128)(2,1)} %bitcast.6) | data formatting | bytes 1835008

commit v3 on v2

--- a/solution.py
+++ b/solution.py
@@ -104,10 +104,10 @@
     length,
     pair_weight,
     partner,
-    norm_gain,
-    final_gain,
-    value_head,
-    qkv_bias,
+    norm_gain_flat,
+    final_gain_flat,
+    value_head_flat,
+    qkv_bias_flat,
     cosine,
     sine,
     hidden,
@@ -127,6 +127,10 @@
     score_tile,
     score_all,
     partner_rows,
+    norm_gain,
+    final_gain,
+    value_head,
+    qkv_bias,
     local_sem,
     recv_sem,
     send_sem,
@@ -199,6 +203,19 @@
             for copy in locals_[m][c]:
                 copy.start()
     tok_local.start()
+    vectors = [
+        pltpu.make_async_copy(flat, row.at[0], local_sem.at[count + 1 + i])
+        for i, (flat, row) in enumerate(
+            (
+                (norm_gain_flat, norm_gain),
+                (final_gain_flat, final_gain),
+                (value_head_flat, value_head),
+                (qkv_bias_flat, qkv_bias),
+            )
+        )
+    ]
+    for copy in vectors:
+        copy.start()
 
     barrier = pltpu.get_barrier_semaphore()
     across = 2 * z + 1 - y
@@ -302,6 +319,8 @@
         own_line(1, c)
 
     tok_local.wait()
+    for copy in vectors:
+        copy.wait()
     for peer in peers:
         pltpu.make_async_copy(tok_all.at[peer], tok_all.at[peer], tok_recv.at[peer]).wait()
         pltpu.make_async_copy(len_all.at[peer], len_all.at[peer], len_recv.at[peer]).wait()
@@ -579,7 +598,7 @@
             jax.ShapeDtypeStruct((1,), f32),
             jax.ShapeDtypeStruct((1,), f32),
         ),
-        in_specs=[anywhere] * 3 + [scalar] * 3 + [vmem] * 6,
+        in_specs=[anywhere] * 3 + [scalar] * 3 + [anywhere] * 4 + [vmem] * 2,
         out_specs=(vmem, scalar, scalar),
         scratch_shapes=[
             pltpu.VMEM((shards * depth, all_cols), bf16),
@@ -596,7 +615,11 @@
             pltpu.VMEM((8, HEAD_SIZE), f32),
             pltpu.VMEM((everyone, 8, HEAD_SIZE), f32),
             pltpu.VMEM((everyone, HEAD_SIZE), jnp.int32),
-            dma((10,)),
+            pltpu.VMEM((1, width), f32),
+            pltpu.VMEM((1, width), f32),
+            pltpu.VMEM((1, width), f32),
+            pltpu.VMEM((1, qkv_bias.shape[0]), f32),
+            dma((13,)),
             dma((2, 2, shards)),
             dma((3, 2, 2, shards)),
             dma((groups,)),
@@ -618,10 +641,10 @@
         lengths,
         pair_weight,
         partner,
-        norm_gain[None],
-        final_gain[None],
-        value_head[None],
-        qkv_bias[None],
+        norm_gain,
+        final_gain,
+        value_head,
+        qkv_bias,
         jnp.asarray(cosine),
         jnp.asarray(sine),
     )

time: 191 us -> 186 us (0.974)
  local copies, waits for them, and re-layouts: 7.48 us -> 2.16 us
    broadcast_in_dim x4 -> x0, local copies, waits for them, and re-layouts: 5.32 us -> none  [the longest x1 1.35 us: layer(): qkv_bias[None]]
where the time goes in v3:
time: 186 us
  Pallas kernels  178 us (96%)
  between operations  5.48 us (3%)
  local copies, waits for them, and re-layouts  2.16 us (1%)
    pallas_call x1, Pallas kernels, layer(): pl.pallas_call(functools.partial(layer_kernel, shards, groups), out_shape...  178 us

profile of v3, /device:TPU:0, one launch (start us, length us, event | category | flops | bytes accessed | tf_op | source)
XLA Modules:
  0.0 185.7 jit_solution(12749694540796976451)
XLA Ops:
  1.9 178.1 %shard_map.139 = (bf16[128,3584]{1,0:T(8,128)(2,1)}, f32[1]{0:T(128)}, f32[1]{0:T(128)}) custom-call(bf16[128,3584]{1,0:T(8,128)(2,1)} %bitcast.5, bf16[448,4608]{1,0:T(8,128)(2,1)} %qkv_weight.1, bf16[448,3584]{1,0:T(8,128)(2,1)} %bitcast.4, s32[1]{0:T(128)S(6)} %copy.18.length, f32[1]{0:T(128)S(6)} %copy.19.pair_weight, s32[32]{0:T(128)} %partner.1, ...), custom_call_target="tpu_custom_call" | custom-call | tf_op jit(solution)/shard_map/pallas_call | solution.py:594
  180.0 2.2 %copy.20 = bf16[1,128,3584]{2,1,0:T(8,128)(2,1)} copy(bf16[1,128,3584]{2,1,0:T(8,128)(2,1)} %bitcast.6) | data formatting | bytes 1835008
